TPU v7x, 256 devices: a whole 4x4x8 slice. The times are simulated.
256 devices in a mesh: slab: 16 (over y_hi, z), sub: 16 (over x, y_lo, core).
Axes of the slice: x: 4, y: 4 (y_hi: 2, y_lo: 2; y = y_hi * 2 + y_lo), z: 8, core: 2. Of those that a mesh axis runs over, the one named last changes fastest.
Arguments:
- features: bfloat16 [64, 256, 49, 128], P('slab', 'sub'), may hold values from -6 to 6
- source_cell: int32 [16, 16, 2, 128], P('slab', 'sub'), may hold values from 42 to 117, as said below
- target_cell: int32 [16, 16, 2, 128], P('slab', 'sub'), may hold values from 0 to 159, as said below
- rotation: bfloat16 [16, 16, 2, 128, 455], P('slab', 'sub'), may hold values from -4 to 4
- edge_count: int32 [16, 16], P('slab', 'sub'), may hold values from 64 to 256, as said below
- first_zero: bfloat16 [896, 896], replicated, may hold values from -0.1875 to 0.1875
- first_one: bfloat16 [2, 768, 768], replicated, may hold values from -0.15625 to 0.15625
- first_two: bfloat16 [2, 640, 640], replicated, may hold values from -0.15625 to 0.15625
- second_zero: bfloat16 [896, 896], replicated, may hold values from -0.1875 to 0.1875
- second_one: bfloat16 [2, 768, 768], replicated, may hold values from -0.15625 to 0.15625
- second_two: bfloat16 [2, 640, 640], replicated, may hold values from -0.15625 to 0.15625
Outputs:
- aggregated: bfloat16 [64, 256, 49, 128], P('slab', 'sub')
Inputs may be any that keep to these rules, and one draw needn't show every extreme that they name: source_cell names an atom of the device's own 4 x 16 block, as a cell of its window numbered row by row. target_cell names an atom other than the source, at most 2 atom rows and 2 atom columns from it. Slots at positions edge_count and beyond are unused; in every draw some device holds 256 live slots.
All inputs are finite; a program needn't handle non-finite values.
Results may differ from a plain program's by a relative error of at most 0.0074.
Values may be sent and summed in bfloat16 or wider, within the bound.
A program may use at most 128 MiB of HBM per device.

v0:
```python
import math

import jax
import jax.numpy as jnp
from jax import lax
from jax.sharding import PartitionSpec as P

DEGREE = 6
REACH = 2


exact_mode = lax.Precision.HIGHEST


def shifted(block, axis, distance):
    devices = range(lax.axis_size(axis))
    route = [((i - distance) % len(devices), i) for i in devices]
    return lax.ppermute(block, axis, route)


def extended(block, sides, width):
    for axis, dim in sides:
        count = lax.axis_size(axis)
        forward = [(i, i + 1) for i in range(count - 1)]
        forward.append((count - 1, 0))
        backward = [(target, source) for source, target in forward]
        low = lax.ppermute(
            lax.slice_in_dim(block, block.shape[dim] - width, None, axis=dim), axis, forward
        )
        high = lax.ppermute(lax.slice_in_dim(block, 0, width, axis=dim), axis, backward)
        block = jnp.concatenate([low, block, high], axis=dim)
    return block


def block_of(frames, degree):
    offset = sum(((2 * lower_degree + 1) ** 2 for lower_degree in range(degree)))
    block_width = 2 * degree + 1
    return frames[:, offset : offset + block_width * block_width].reshape(
        frames.shape[0], block_width, block_width
    )


def turn_in(edge_input, frames):
    edge_rows = edge_input.shape[0]
    zero_rows, plus_one, minus_one, plus_two, minus_two = ([], [], [], [], [])
    for degree in range(DEGREE + 1):
        wigner_piece = block_of(frames, degree)
        inputs_piece = edge_input[:, degree * degree : (degree + 1) * (degree + 1), :]
        turned = jnp.einsum(
            "eij,ejc->eic", wigner_piece, inputs_piece, preferred_element_type=jnp.float32
        ) / math.sqrt(2 * degree + 1)
        zero_rows.append(turned[:, degree])
        if degree >= 1:
            plus_one.append(turned[:, degree + 1])
            minus_one.append(turned[:, degree - 1])
        if degree >= 2:
            plus_two.append(turned[:, degree + 2])
            minus_two.append(turned[:, degree - 2])
    order_zero = jnp.stack(zero_rows, 1).reshape(edge_rows, -1).astype(jnp.bfloat16)
    order_one = (
        jnp.concatenate([jnp.stack(plus_one, 1), jnp.stack(minus_one, 1)], 0)
        .reshape(2 * edge_rows, -1)
        .astype(jnp.bfloat16)
    )
    order_two = (
        jnp.concatenate([jnp.stack(plus_two, 1), jnp.stack(minus_two, 1)], 0)
        .reshape(2 * edge_rows, -1)
        .astype(jnp.bfloat16)
    )
    return (order_zero, order_one, order_two)


def convolve(order_zero, order_one, order_two, w_zero, w_one, w_two):
    edge_rows = order_zero.shape[0]
    results = [jnp.dot(order_zero, w_zero, preferred_element_type=jnp.float32)]
    for pair_in, w_pair in ((order_one, w_one), (order_two, w_two)):
        former = jnp.dot(pair_in, w_pair[0], preferred_element_type=jnp.float32)
        latter = jnp.dot(pair_in, w_pair[1], preferred_element_type=jnp.float32)
        results.append(former[:edge_rows] - latter[edge_rows:])
        results.append(former[edge_rows:] + latter[:edge_rows])
    return results


def activate(results, channels):
    edge_rows = results[0].shape[0]
    zero_part = results[0].reshape(edge_rows, -1, channels)
    scalar = zero_part[:, 0]
    gating = jax.nn.sigmoid(scalar)[:, None, :]
    zero_part = jnp.concatenate([jax.nn.silu(scalar)[:, None, :], zero_part[:, 1:] * gating], 1)
    shaped = [piece_out.reshape(edge_rows, -1, channels) * gating for piece_out in results[1:]]
    order_zero = zero_part.reshape(edge_rows, -1).astype(jnp.bfloat16)
    order_one = (
        jnp.concatenate([shaped[0], shaped[1]], 0).reshape(2 * edge_rows, -1).astype(jnp.bfloat16)
    )
    order_two = (
        jnp.concatenate([shaped[2], shaped[3]], 0).reshape(2 * edge_rows, -1).astype(jnp.bfloat16)
    )
    return (order_zero, order_one, order_two)


def turn_out(results, frames, channels):
    edge_rows = results[0].shape[0]
    zero_part, plus_one, minus_one, plus_two, minus_two = [
        piece_out.reshape(edge_rows, -1, channels) for piece_out in results
    ]
    pieces = []
    for degree in range(DEGREE + 1):
        row_list = [zero_part[:, degree]]
        if degree >= 1:
            row_list = [minus_one[:, degree - 1]] + row_list + [plus_one[:, degree - 1]]
        if degree >= 2:
            row_list = [minus_two[:, degree - 2]] + row_list + [plus_two[:, degree - 2]]
        spread = len(row_list) // 2
        wigner_piece = block_of(frames, degree).astype(jnp.float32)[
            :, degree - spread : degree + spread + 1, :
        ]
        column = jnp.stack(row_list, 1)
        pieces.append(
            jnp.einsum("eji,ejc->eic", wigner_piece, column, precision=exact_mode)
            / math.sqrt(2 * degree + 1)
        )
    return jnp.concatenate(pieces, 1).astype(jnp.bfloat16)


def message(edge_input, frames, weights):
    channels = edge_input.shape[-1]
    order_zero, order_one, order_two = turn_in(edge_input, frames)
    results = convolve(order_zero, order_one, order_two, weights[0], weights[1], weights[2])
    order_zero, order_one, order_two = activate(results, channels)
    results = convolve(order_zero, order_one, order_two, weights[3], weights[4], weights[5])
    return turn_out(results, frames, channels)


def edge_inputs(window_cells, from_cell, to_cell):
    return (
        window_cells[from_cell].astype(jnp.float32) + window_cells[to_cell].astype(jnp.float32)
    ).astype(jnp.bfloat16)


def deposit(messages, to_cell, is_live, cell_total):
    places = lax.broadcasted_iota(jnp.int32, (cell_total, to_cell.shape[0]), 0)
    one_hot = ((places == to_cell[None, :]) & is_live[None, :]).astype(jnp.bfloat16)
    return jnp.dot(
        one_hot, messages.reshape(messages.shape[0], -1), preferred_element_type=jnp.float32
    )


def fold_columns(folded, own_cols):
    for shift_by in (1, -1):
        if shift_by == 1:
            rim_part = folded[:, own_cols + REACH :]
        else:
            rim_part = folded[:, :REACH]
        arrived = shifted(rim_part, "sub", shift_by)
        if shift_by == 1:
            folded = folded.at[:, REACH : 2 * REACH].add(arrived)
        else:
            folded = folded.at[:, own_cols : own_cols + REACH].add(arrived)
    return folded[:, REACH : REACH + own_cols]


def fold_rows(folded, own_rows):
    for shift_by in (1, -1):
        if shift_by == 1:
            rim_part = folded[own_rows + REACH :]
        else:
            rim_part = folded[:REACH]
        arrived = shifted(rim_part, "slab", shift_by)
        if shift_by == 1:
            folded = folded.at[REACH : 2 * REACH].add(arrived)
        else:
            folded = folded.at[own_rows : own_rows + REACH].add(arrived)
    return folded[REACH : REACH + own_rows]


def fold_back(collected, own_rows, own_cols, components, channels):
    folded = collected.reshape(own_rows + 2 * REACH, own_cols + 2 * REACH, components * channels)
    folded = fold_columns(fold_rows(folded, own_rows), own_cols)
    return folded.reshape(own_rows, own_cols, components, channels).astype(jnp.bfloat16)


def shards(
    features,
    source_cell,
    target_cell,
    rotation,
    edge_count,
    first_zero,
    first_one,
    first_two,
    second_zero,
    second_one,
    second_two,
):
    weights = (first_zero, first_one, first_two, second_zero, second_one, second_two)
    own_rows, own_cols, components, channels = features.shape
    window = extended(features, (("slab", 0), ("sub", 1)), REACH)
    wide_rows = own_rows + 2 * REACH
    wide_cols = own_cols + 2 * REACH
    cell_total = wide_rows * wide_cols
    window_cells = window.reshape(cell_total, components, channels)
    sources = source_cell[0, 0]
    targets = target_cell[0, 0]
    frames_all = rotation[0, 0]
    edge_total = edge_count[0, 0]
    tile_slots, tile_edges = sources.shape
    busy_tiles = (edge_total + tile_edges - 1) // tile_edges
    edge_lane = lax.iota(jnp.int32, tile_edges)

    def one_tile(tile_index, collected):
        from_cell = lax.dynamic_index_in_dim(sources, tile_index, 0, keepdims=False)
        to_cell = lax.dynamic_index_in_dim(targets, tile_index, 0, keepdims=False)
        frames = lax.dynamic_index_in_dim(frames_all, tile_index, 0, keepdims=False)
        is_live = tile_index * tile_edges + edge_lane < edge_total
        messages = message(edge_inputs(window_cells, from_cell, to_cell), frames, weights)
        return collected + deposit(messages, to_cell, is_live, cell_total)

    collected = jnp.zeros((cell_total, components * channels), jnp.float32)
    collected = lax.fori_loop(0, busy_tiles, one_tile, collected)
    return fold_back(collected, own_rows, own_cols, components, channels)


def solution(mesh):
    return jax.shard_map(
        shards,
        mesh=mesh,
        in_specs=(
            P("slab", "sub", None, None),
            P("slab", "sub", None, None),
            P("slab", "sub", None, None),
            P("slab", "sub", None, None, None),
            P("slab", "sub"),
            P(),
            P(),
            P(),
            P(),
            P(),
            P(),
        ),
        out_specs=P("slab", "sub", None, None),
        check_vma=False,
    )
```

profile of v0, /device:TPU:7, one launch (start us, length us, event | category | flops | bytes accessed | tf_op | source)
XLA Modules:
  0.0 238.4 jit_solution(5101835813949857799)
XLA Ops:
  1.3 1.7 collective-permute-start
  3.1 6.7 %collective-permute-start.1 = (bf16[2,16,49,128]{3,1,2,0:T(8,128)(2,1)S(1)}, bf16[2,16,49,128]{3,1,2,0:T(8,128)(2,1)S(1)}, u32[]{:S(2)}, u32[]{:S(2)}) collective-permute-start(bf16[2,16,49,128]{3,1,2,0:T(8,128)(2,1)S(1)} %get-tuple-element.335), channel_id=1, source_target_pairs={{16,0},{32,16},{48,32},{64,48},{80,64},{96,80},{112,96},{128,112},... | collective-permute-start | bytes 1204232 | tf_op jit(solution)/shard_map/ppermute | solution.py:30
  10.0 8.6 %collective-permute-done = bf16[2,16,49,128]{3,1,2,0:T(8,128)(2,1)S(1)} collective-permute-done((bf16[2,16,49,128]{3,1,2,0:T(8,128)(2,1)S(1)}, bf16[2,16,49,128]{3,1,2,0:T(8,128)(2,1)S(1)}, u32[]{:S(2)}, u32[]{:S(2)}) %collective-permute-start) | collective-permute-done | bytes 401440 | tf_op jit(solution)/shard_map/ppermute | solution.py:27
  22.6 2.3 copy.275
  24.9 3.6 %copy.276 = bf16[896,896]{0,1:T(8,128)(2,1)} copy(bf16[896,896]{1,0:T(8,128)(2,1)} %param.29) | data formatting | bytes 3211264
  29.4 2.4 %pad_maximum_fusion.14 = bf16[8,20,49,128]{3,0,2,1:T(8,128)(2,1)S(1)} fusion(bf16[8,2,49,128]{3,0,2,1:T(8,128)(2,1)} %collective-permute-done.3, bf16[2,16,49,128]{3,0,2,1:T(2,128)(2,1)S(1)} %copy.272, bf16[4,16,49,128]{3,0,2,1:T(4,128)(2,1)S(1)} %copy.271, bf16[2,16,49,128]{3,0,2,1:T(2,128)(2,1)S(1)} %copy.270, ...), kind=kLoop, calls=%fused_computation.192 | loop fusion | flops 10035200 | bytes 4014080 | tf_op jit(solution)/shard_map/concatenate | solution.py:31
  32.2 2.2 broadcast_in_dim.2
  34.4 64.6 %while.15 = (s32[]{:T(128)}, f32[160,6272]{1,0:T(8,128)}, s32[]{:T(128)}, s32[2,128]{1,0:T(2,128)}, s32[]{:T(128)}, /*index=5*/bf16[2,128,455]{1,2,0:T(8,128)(2,...) while((s32[]{:T(128)}, f32[160,6272]{1,0:T(8,128)}, ...), condition=%wide.region_1.2_spmd.clone, body=%wide.region_0.1_spmd.clone.sunk | while | flops 2790833408 | bytes 180411008 | solution.py:219
  35.1 2.0 gather_fusion
  37.2 2.1 gather_fusion.1
  39.3 2.5 %add_convert_fusion.2 = bf16[128,49,128]{2,1,0:T(8,128)(2,1)S(1)} fusion(bf16[128,49,128]{2,1,0:T(8,128)(2,1)} %gather_fusion, bf16[128,49,128]{2,1,0:T(8,128)(2,1)} %gather_fusion.1), kind=kLoop, calls=%fused_computation.4.clone.1 | loop fusion | flops 3211264 | bytes 4816896 | tf_op jit(solution)/shard_map/while/body/convert_element_type | solution.py:137
  56.6 2.8 %fusion.262 = f32[256,768]{1,0:T(8,128)} fusion(bf16[2,768,768]{2,1,0:T(8,128)(2,1)} %get-tuple-element.606, bf16[128,768]{0,1:T(8,128)(2,1)S(1)} %bitcast.249, bf16[128,768]{0,1:T(8,128)(2,1)S(1)} %bitcast.251), kind=kOutput, calls=%fused_computation.11.clone.1 | convolution fusion | flops 302776320 | bytes 2359296 | tf_op jit(solution)/shard_map/while/body/dot_general | solution.py:77
  65.4 2.6 %fusion.257 = f32[256,640]{1,0:T(8,128)} fusion(bf16[2,640,640]{2,1,0:T(8,128)(2,1)} %get-tuple-element.608, bf16[128,640]{0,1:T(8,128)(2,1)S(1)} %bitcast.253, bf16[128,640]{0,1:T(8,128)(2,1)S(1)} %bitcast.255), kind=kOutput, calls=%fused_computation.27.clone.1 | convolution fusion | flops 210370560 | bytes 1802240 | tf_op jit(solution)/shard_map/while/body/dot_general | solution.py:77
  89.7 2.5 %copy.421 = bf16[128,49,128]{0,2,1:T(8,128)(2,1)} copy(bf16[128,49,128]{2,0,1:T(8,128)(2,1)S(1)} %fusion.278) | data formatting | bytes 3211264 | tf_op jit(solution)/shard_map/while/body/concatenate | solution.py:122
  93.6 5.4 %convolution_add_fusion.2 = f32[160,6272]{1,0:T(8,128)} fusion(f32[160,6272]{1,0:T(8,128)} %get-tuple-element.579, bf16[128,6272]{0,1:T(8,128)(2,1)} %bitcast.237, s32[128]{0:T(128)S(1)} %fusion.279, pred[128]{0:T(512)(128)(4,1)S(1)} %fusion.280), kind=kOutput, calls=%fused_computation.3.clone.1 | convolution fusion | flops 257945600 | bytes 9634432 | tf_op jit(solution)/shard_map/while/body/dot_general | solution.py:143
  99.0 1.6 fusion.97
  101.3 5.0 %reshape.295 = f32[8,20,6272]{2,1,0:T(8,128)} reshape(f32[160,6272]{1,0:T(8,128)} %get-tuple-element.131) | data formatting | bytes 8028160 | tf_op jit(solution)/shard_map/reshape | solution.py:177
  106.4 11.8 %collective-permute-done.4 = f32[2,20,6272]{2,0,1:T(2,128)} collective-permute-done((f32[2,20,6272]{2,0,1:T(2,128)S(1)}, f32[2,20,6272]{2,0,1:T(2,128)}, u32[]{:S(2)}, u32[]{:S(2)}) %collective-permute-start.4) | collective-permute-done | bytes 1003552 | tf_op jit(solution)/shard_map/ppermute | solution.py:18
  118.2 2.4 fusion.93
  123.8 86.2 %collective-permute-done.5 = f32[2,20,6272]{2,0,1:T(2,128)S(1)} collective-permute-done((f32[2,20,6272]{2,0,1:T(2,128)S(1)}, f32[2,20,6272]{2,0,1:T(2,128)S(1)}, u32[]{:S(2)}, u32[]{:S(2)}) %collective-permute-start.5) | collective-permute-done | bytes 1003552 | tf_op jit(solution)/shard_map/ppermute | solution.py:18
  210.0 2.5 %fusion.92 = f32[8,20,6272]{2,1,0:T(8,128)} fusion(f32[8,20,6272]{2,1,0:T(8,128)} %fusion.93, f32[2,20,6272]{2,0,1:T(2,128)S(1)} %collective-permute-done.5), kind=kLoop, calls=%fused_computation.195 | loop fusion | flops 250880 | bytes 3411968 | tf_op jit(solution)/shard_map/scatter-add | solution.py:172
  213.7 13.4 %collective-permute-start.6 = (f32[4,2,6272]{2,1,0:T(2,128)S(1)}, f32[4,2,6272]{2,1,0:T(2,128)S(1)}, u32[]{:S(2)}, u32[]{:S(2)}) collective-permute-start(f32[4,2,6272]{2,1,0:T(2,128)S(1)} %slice.688), channel_id=1, source_target_pairs={{15,0},{0,1},{1,2},{2,3},{3,4},{4,5},{5,6},{6,7},{7,8},{8,9},{9,10... | collective-permute-start | bytes 602120 | tf_op jit(solution)/shard_map/ppermute | solution.py:18
  227.1 1.8 slice.686
  231.2 5.9 %collective-permute-done.7 = f32[4,2,6272]{2,1,0:T(2,128)S(1)} collective-permute-done((f32[4,2,6272]{2,1,0:T(2,128)S(1)}, f32[4,2,6272]{2,1,0:T(2,128)S(1)}, u32[]{:S(2)}, u32[]{:S(2)}) %collective-permute-start.7) | collective-permute-done | bytes 200736 | tf_op jit(solution)/shard_map/ppermute | solution.py:18
  (191 shorter events, 58.8 us)
Async XLA Ops:
  0.0 9.7 %copy-start.21 = (bf16[4,16,49,128]{3,1,2,0:T(8,128)(2,1)S(1)}, bf16[4,16,49,128]{3,1,2,0:T(8,128)(2,1)}, u32[]{:S(2)}) copy-start(bf16[4,16,49,128]{3,1,2,0:T(8,128)(2,1)} %param.21) | copy-start | bytes 2408452
  1.3 17.3 %collective-permute-start = (bf16[2,16,49,128]{3,1,2,0:T(8,128)(2,1)S(1)}, bf16[2,16,49,128]{3,1,2,0:T(8,128)(2,1)S(1)}, u32[]{:S(2)}, u32[]{:S(2)}) collective-permute-start(bf16[2,16,49,128]{3,1,2,0:T(8,128)(2,1)S(1)} %get-tuple-element.334), channel_id=1, source_target_pairs={{0,16},{16,32},{32,48},{48,64},{64,80},{80,96},{96,112},{112,128},... | collective-permute-start | bytes 1204232 | tf_op jit(solution)/shard_map/ppermute | solution.py:27
  3.1 15.9 %collective-permute-start.1 = (bf16[2,16,49,128]{3,1,2,0:T(8,128)(2,1)S(1)}, bf16[2,16,49,128]{3,1,2,0:T(8,128)(2,1)S(1)}, u32[]{:S(2)}, u32[]{:S(2)}) collective-permute-start(bf16[2,16,49,128]{3,1,2,0:T(8,128)(2,1)S(1)} %get-tuple-element.335), channel_id=1, source_target_pairs={{16,0},{32,16},{48,32},{64,48},{80,64},{96,80},{112,96},{128,112},... | collective-permute-start | bytes 1204232 | tf_op jit(solution)/shard_map/ppermute | solution.py:30
  10.0 12.5 %copy-start.24 = (bf16[896,896]{1,0:T(8,128)(2,1)S(1)}, bf16[896,896]{1,0:T(8,128)(2,1)}, u32[]{:S(2)}) copy-start(bf16[896,896]{1,0:T(8,128)(2,1)} %param.26) | copy-start | bytes 4816900
  20.3 8.2 %collective-permute-start.2 = (bf16[8,2,49,128]{3,0,2,1:T(8,128)(2,1)}, bf16[8,2,49,128]{3,0,2,1:T(8,128)(2,1)S(1)}, u32[]{:S(2)}, u32[]{:S(2)}) collective-permute-start(bf16[8,2,49,128]{3,0,2,1:T(8,128)(2,1)} %get-tuple-element.332), channel_id=1, source_target_pairs={{0,1},{1,2},{2,3},{3,4},{4,5},{5,6},{6,7},{7,8},{8,9},{9,10},{10,1... | collective-permute-start | bytes 602120 | tf_op jit(solution)/shard_map/ppermute | solution.py:27
  21.9 7.5 %collective-permute-start.3 = (bf16[8,2,49,128]{3,0,2,1:T(8,128)(2,1)}, bf16[8,2,49,128]{3,0,2,1:T(8,128)(2,1)}, u32[]{:S(2)}, u32[]{:S(2)}) collective-permute-start(bf16[8,2,49,128]{3,0,2,1:T(8,128)(2,1)} %get-tuple-element.333), channel_id=1, source_target_pairs={{1,0},{2,1},{3,2},{4,3},{5,4},{6,5},{7,6},{8,7},{9,8},{10,9},{11,1... | collective-permute-start | bytes 602120 | tf_op jit(solution)/shard_map/ppermute | solution.py:30
  24.9 3.6 %copy-start.25 = (bf16[1,1,2,128,455]{3,2,4,1,0:T(2,128)(2,1)S(1)}, bf16[1,1,2,128,455]{3,2,4,1,0:T(2,128)(2,1)}, u32[]{:S(2)}) copy-start(bf16[1,1,2,128,455]{3,2,4,1,0:T(2,128)(2,1)} %param.24) | copy-start | bytes 698884
  34.4 2.8 %copy-start = (bf16[160,49,128]{2,1,0:T(8,128)(2,1)}, bf16[160,49,128]{2,1,0:T(8,128)(2,1)S(1)}, u32[]{:S(2)}) copy-start(bf16[160,49,128]{2,1,0:T(8,128)(2,1)S(1)} %get-tuple-element.603) | copy-start | bytes 6021124 | tf_op jit(solution)/shard_map/while
  34.4 7.4 %copy-start.22 = (bf16[2,128,455]{1,2,0:T(8,128)(2,1)}, bf16[2,128,455]{1,2,0:T(8,128)(2,1)S(1)}, u32[]{:S(2)}) copy-start(bf16[2,128,455]{1,2,0:T(8,128)(2,1)S(1)} %get-tuple-element.601) | copy-start | bytes 698884 | tf_op jit(solution)/shard_map/while
  56.6 2.8 %copy-start.28 = (bf16[2,768,768]{2,1,0:T(8,128)(2,1)S(1)}, bf16[2,768,768]{2,1,0:T(8,128)(2,1)}, u32[]{:S(2)}) copy-start(bf16[2,768,768]{2,1,0:T(8,128)(2,1)} %get-tuple-element.606) | copy-start | bytes 7077892 | tf_op jit(solution)/shard_map/while
  61.0 2.1 copy-start.29
  65.4 2.6 %copy-start.30 = (bf16[2,640,640]{2,1,0:T(8,128)(2,1)S(1)}, bf16[2,640,640]{2,1,0:T(8,128)(2,1)}, u32[]{:S(2)}) copy-start(bf16[2,640,640]{2,1,0:T(8,128)(2,1)} %get-tuple-element.608) | copy-start | bytes 4915204 | tf_op jit(solution)/shard_map/while
  76.5 2.7 %copy-start.7 = (bf16[128,3,3]{1,2,0:T(4,128)(2,1)S(1)}, bf16[128,3,3]{1,2,0:T(4,128)(2,1)}, u32[]{:S(2)}) copy-start(bf16[128,3,3]{1,2,0:T(4,128)(2,1)} %copy-done.6) | copy-start | bytes 6916 | tf_op jit(solution)/shard_map/while
  77.2 2.6 %copy-start.27 = (f32[128]{0:T(128)S(1)}, f32[128]{0:T(128)}, u32[]{:S(2)}) copy-start(f32[128]{0:T(128)} %copy-done.26) | copy-start | bytes 1540 | tf_op jit(solution)/shard_map/while
  78.4 3.6 %copy-start.14 = (f32[128,5,128]{0,2,1:T(8,128)S(1)}, f32[128,5,128]{0,2,1:T(8,128)}, u32[]{:S(2)}) copy-start(f32[128,5,128]{0,2,1:T(8,128)} %get-tuple-element.556) | copy-start | bytes 983044 | tf_op jit(solution)/shard_map/while
  81.2 2.6 %copy-start.12 = (f32[128,5,128]{0,2,1:T(8,128)S(1)}, f32[128,5,128]{0,2,1:T(8,128)}, u32[]{:S(2)}) copy-start(f32[128,5,128]{0,2,1:T(8,128)} %get-tuple-element.557) | copy-start | bytes 983044 | tf_op jit(solution)/shard_map/while
  83.8 1.9 copy-start.10
  86.0 2.7 %copy-start.5 = (bf16[128,13,13]{2,1,0:T(8,128)(2,1)S(1)}, bf16[128,13,13]{2,1,0:T(8,128)(2,1)}, u32[]{:S(2)}) copy-start(bf16[128,13,13]{2,1,0:T(8,128)(2,1)} %copy.401) | copy-start | bytes 129796 | tf_op jit(solution)/shard_map/while
  93.6 5.4 %copy-start.1 = (bf16[160,49,128]{2,1,0:T(8,128)(2,1)S(1)}, bf16[160,49,128]{2,1,0:T(8,128)(2,1)}, u32[]{:S(2)}) copy-start(bf16[160,49,128]{2,1,0:T(8,128)(2,1)} %copy-done) | copy-start | bytes 6021124 | tf_op jit(solution)/shard_map/while
  93.6 5.4 %copy-start.23 = (bf16[2,128,455]{1,2,0:T(8,128)(2,1)S(1)}, bf16[2,128,455]{1,2,0:T(8,128)(2,1)}, u32[]{:S(2)}) copy-start(bf16[2,128,455]{1,2,0:T(8,128)(2,1)} %copy-done.22) | copy-start | bytes 698884 | tf_op jit(solution)/shard_map/while
  101.2 17.0 %collective-permute-start.4 = (f32[2,20,6272]{2,0,1:T(2,128)S(1)}, f32[2,20,6272]{2,0,1:T(2,128)}, u32[]{:S(2)}, u32[]{:S(2)}) collective-permute-start(f32[2,20,6272]{2,0,1:T(2,128)S(1)} %copy.277), channel_id=1, source_target_pairs={{240,0},{0,16},{16,32},{32,48},{48,64},{64,80},{80,96},{96,112},{1... | collective-permute-start | bytes 3010568 | tf_op jit(solution)/shard_map/ppermute | solution.py:18
  122.5 87.5 %collective-permute-start.5 = (f32[2,20,6272]{2,0,1:T(2,128)S(1)}, f32[2,20,6272]{2,0,1:T(2,128)S(1)}, u32[]{:S(2)}, u32[]{:S(2)}) collective-permute-start(f32[2,20,6272]{2,0,1:T(2,128)S(1)} %copy.279), channel_id=1, source_target_pairs={{16,0},{32,16},{48,32},{64,48},{80,64},{96,80},{112,96},{128,112},... | collective-permute-start | bytes 3010568 | tf_op jit(solution)/shard_map/ppermute | solution.py:18
  213.7 16.0 %collective-permute-start.6 = (f32[4,2,6272]{2,1,0:T(2,128)S(1)}, f32[4,2,6272]{2,1,0:T(2,128)S(1)}, u32[]{:S(2)}, u32[]{:S(2)}) collective-permute-start(f32[4,2,6272]{2,1,0:T(2,128)S(1)} %slice.688), channel_id=1, source_target_pairs={{15,0},{0,1},{1,2},{2,3},{3,4},{4,5},{5,6},{6,7},{7,8},{8,9},{9,10... | collective-permute-start | bytes 602120 | tf_op jit(solution)/shard_map/ppermute | solution.py:18
  231.2 6.0 %collective-permute-start.7 = (f32[4,2,6272]{2,1,0:T(2,128)S(1)}, f32[4,2,6272]{2,1,0:T(2,128)S(1)}, u32[]{:S(2)}, u32[]{:S(2)}) collective-permute-start(f32[4,2,6272]{2,1,0:T(2,128)S(1)} %slice.690), channel_id=1, source_target_pairs={{1,0},{2,1},{3,2},{4,3},{5,4},{6,5},{7,6},{8,7},{9,8},{10,9},{11,1... | collective-permute-start | bytes 602120 | tf_op jit(solution)/shard_map/ppermute | solution.py:18
  (16 other events, 18.0 us)
where the time goes:
time: 240 us; the launch traced here: 238 us
  waiting for transfers between devices  114 us (48%)
  local copies, waits for them, and re-layouts  50.8 us (21%)
  starting transfers between devices  24.8 us (10%)
  other arithmetic  23.7 us (10%)
  matrix products  23.5 us (10%)
    ppermute x4, waiting for transfers between devices, shifted(): return lax.ppermute(block, axis, route)  105 us
    ppermute x4, starting transfers between devices, shifted(): return lax.ppermute(block, axis, route)  14.8 us
    while x69, local copies, waits for them, and re-layouts  8.9 us
    ppermute x2, waiting for transfers between devices, extended(): lax.ppermute(lax.slice_in_dim(block, block.shape[dim] - width, None, axis...  8.58 us
    ppermute x2, starting transfers between devices, extended(): lax.ppermute(lax.slice_in_dim(block, 0, width, axis=dim), axis, backward)  6.66 us
    unnamed x11, local copies, waits for them, and re-layouts  6.63 us
    dot_general x4, matrix products, convolve(): former = jnp.dot(pair_in, w_pair[0], preferred_element_type=jnp.float32)  6.32 us
    dot_general x1, matrix products, deposit(): jnp.dot(one_hot, messages.reshape(messages.shape[0], -1), preferred_eleme...  5.36 us
  transfers between devices with their start and end apart: 8, of which 6 were waited for; matrix products, arithmetic and copies ran while one was open for 6% of the time, Pallas kernels for 0%

commit v1 on v0

v1 whole, which is shorter than its diff:
```python
import math

import jax
import jax.numpy as jnp
import numpy as np
from jax import lax
from jax.experimental import pallas as pl
from jax.experimental.pallas import tpu as pltpu
from jax.sharding import PartitionSpec as P

DEGREE = 6
REACH = 2
COMPS = 49
WIGNER = 455
EDGES = 256
GROUP = 16
GROUPS = EDGES // GROUP
BF = jnp.bfloat16
F32 = jnp.float32


def spread_of(degree):
    return min(degree, 2)


def kept(degree):
    return 2 * spread_of(degree) + 1


FIRST_KEPT = [sum(kept(k) for k in range(d)) for d in range(DEGREE + 2)]
OFFSETS = [sum((2 * k + 1) ** 2 for k in range(d)) for d in range(DEGREE + 1)]


def entry_tables():
    inward = np.full((512,), -1, np.int32)
    outward = np.full((512,), -1, np.int32)
    row = 0
    for degree in range(DEGREE + 1):
        width = 2 * degree + 1
        spread = spread_of(degree)
        for slot, i in enumerate(range(degree - spread, degree + spread + 1)):
            for j in range(width):
                entry = OFFSETS[degree] + i * width + j
                inward[16 * row + j] = entry
                outward[8 * (degree * degree + j) + slot] = entry
            row += 1
    return np.concatenate([inward, outward])[None, :]


def transposed_dot(a, b):
    return lax.dot_general(a, b, (((0,), (0,)), ((), ())), preferred_element_type=F32)


def dot(a, b):
    return jnp.dot(a, b, preferred_element_type=F32)


def expand_rotations(table_ref, turn_ref, padded, grid_map, into, outof):
    wanted = table_ref[...]
    rows = lax.broadcasted_iota(jnp.int32, (WIGNER, 1024), 0)
    pick = jnp.where(rows == wanted, 1.0, 0.0).astype(BF)
    padded[...] = transposed_dot(turn_ref[...], pick).astype(BF)
    k = lax.broadcasted_iota(jnp.int32, (128, 2048), 0)
    col = lax.broadcasted_iota(jnp.int32, (128, 2048), 1)
    grid_map[...] = jnp.where(k == (col >> 4), 1.0, 0.0).astype(BF)
    edge = lax.broadcasted_iota(jnp.int32, (EDGES, 256), 0)
    lane = lax.broadcasted_iota(jnp.int32, (EDGES, 256), 1)
    own = (edge & 15) == (lane & 15)
    for degree in range(DEGREE + 1):
        lanes = 128 if degree <= 3 else 256
        for slot in range(kept(degree)):
            row = FIRST_KEPT[degree] + slot
            block = dot(
                padded[:, 128 * (row // 8) : 128 * (row // 8) + 128],
                grid_map[:, 256 * (row % 8) : 256 * (row % 8) + lanes],
            )
            into[degree][slot] = jnp.where(own[:, :lanes], block, 0.0).astype(BF)
    for pair in range((COMPS + 1) // 2):
        chunk, place = pair // 8, pair % 8
        block = dot(
            padded[:, 512 + 128 * chunk : 640 + 128 * chunk],
            grid_map[:, 256 * place : 256 * place + 256],
        )
        block = jnp.where(own, block, 0.0).astype(BF)
        outof[2 * pair] = block[:, :128]
        if 2 * pair + 1 < COMPS:
            outof[2 * pair + 1] = block[:, 128:]


def cell_numbers(shape):
    k = lax.broadcasted_iota(jnp.int32, shape, 0)
    own = ((k >> 4) + 2) * 20 + (k & 15) + 2
    r = (k - 64) >> 4
    slab = (jnp.where(r < 2, r, r + 4)) * 20 + (k & 15) + 2
    s = (k - 128) & 15
    side = (s >> 1) * 20 + (s & 1) + jnp.where(k >= 144, 18, 0)
    return jnp.where(k < 64, own, jnp.where(k < 128, slab, side))


def compute_kernel(
    own_ref,
    slab_ref,
    left_ref,
    right_ref,
    source_ref,
    target_ref,
    turn_ref,
    count_ref,
    table_ref,
    w0_hbm,
    w1_hbm,
    w2_hbm,
    w3_hbm,
    w4_hbm,
    w5_hbm,
    own_out,
    slab_out,
    left_out,
    right_out,
    w0,
    w1,
    w2,
    w3,
    w4,
    w5,
    padded,
    grid_map,
    i0,
    i1,
    i2,
    i3,
    i4,
    i5,
    i6,
    outof,
    gather_map,
    edges,
    zero_in,
    one_in,
    two_in,
    turned,
    sem,
):
    into = (i0, i1, i2, i3, i4, i5, i6)
    copies = [
        pltpu.make_async_copy(src, dst, sem.at[n])
        for n, (src, dst) in enumerate(
            ((w0_hbm, w0), (w1_hbm, w1), (w2_hbm, w2), (w3_hbm, w3), (w4_hbm, w4), (w5_hbm, w5))
        )
    ]
    for copy in copies:
        copy.start()
    expand_rotations(table_ref, turn_ref, padded, grid_map, into, outof)
    cells = cell_numbers((160, EDGES))
    to_target = jnp.where(cells == target_ref[...], 1.0, 0.0)
    both = to_target + jnp.where(cells == source_ref[...], 1.0, 0.0)
    gather_map[...] = both.T.astype(BF)

    def gather(step, carry):
        pieces = []
        for n in range(7):
            comp = step * 7 + n
            pieces.append(
                jnp.concatenate(
                    [
                        own_ref[:, comp].reshape(64, 128),
                        slab_ref[:, comp].reshape(64, 128),
                        left_ref[comp],
                        right_ref[comp],
                    ],
                    0,
                )
            )
        total = dot(gather_map[...], jnp.concatenate(pieces, 1)).astype(BF)
        for n in range(7):
            edges[step * 7 + n] = total[:, 128 * n : 128 * n + 128]
        return carry

    lax.fori_loop(0, 7, gather, 0)

    def turn_in(group, carry):
        at = pl.ds(pl.multiple_of(group * GROUP, GROUP), GROUP)
        low = pl.ds(pl.multiple_of(EDGES + group * GROUP, GROUP), GROUP)
        for degree in range(DEGREE + 1):
            width = 2 * degree + 1
            n = kept(degree)
            rows = edges[degree * degree : degree * degree + width, at, :]
            result = dot(
                into[degree][:, at, :].reshape(n * GROUP, -1)[:, : width * GROUP],
                rows.reshape(width * GROUP, 128),
            )
            result = result * (1.0 / math.sqrt(width))
            piece = [result[GROUP * k : GROUP * k + GROUP] for k in range(n)]
            mid = n // 2
            zero_in[at, 128 * degree : 128 * degree + 128] = piece[mid].astype(BF)
            if degree >= 1:
                c = 128 * (degree - 1)
                plus, minus = piece[mid + 1].astype(BF), piece[mid - 1]
                one_in[at, c : c + 128] = plus
                one_in[at, 768 + c : 896 + c] = (-minus).astype(BF)
                one_in[low, c : c + 128] = minus.astype(BF)
                one_in[low, 768 + c : 896 + c] = plus
            if degree >= 2:
                c = 128 * (degree - 2)
                plus, minus = piece[mid + 2].astype(BF), piece[mid - 2]
                two_in[at, c : c + 128] = plus
                two_in[at, 640 + c : 768 + c] = (-minus).astype(BF)
                two_in[low, c : c + 128] = minus.astype(BF)
                two_in[low, 640 + c : 768 + c] = plus
        return carry

    lax.fori_loop(0, GROUPS, turn_in, 0)
    for copy in copies[:3]:
        copy.wait()
    y0 = dot(zero_in[...], w0[...])
    scalar = y0[:, :128]
    gate = jax.nn.sigmoid(scalar)
    y1 = dot(one_in[...], w1[...])
    zero_in[:, :128] = (scalar * gate).astype(BF)
    for degree in range(1, DEGREE + 1):
        c = 128 * degree
        zero_in[:, c : c + 128] = (y0[:, c : c + 128] * gate).astype(BF)
    y2 = dot(two_in[...], w2[...])
    for y, ref, half in ((y1, one_in, 768), (y2, two_in, 640)):
        for c in range(0, half, 128):
            plus = y[:EDGES, c : c + 128] * gate
            minus = y[EDGES:, c : c + 128] * gate
            ref[:EDGES, c : c + 128] = plus.astype(BF)
            ref[:EDGES, half + c : half + c + 128] = (-minus).astype(BF)
            ref[EDGES:, c : c + 128] = minus.astype(BF)
            ref[EDGES:, half + c : half + c + 128] = plus.astype(BF)
    for copy in copies[3:]:
        copy.wait()
    u = dot(zero_in[...], w3[...])
    for degree in range(DEGREE + 1):
        scale = 1.0 / math.sqrt(2 * degree + 1)
        at = FIRST_KEPT[degree] + spread_of(degree)
        turned[at] = (u[:, 128 * degree : 128 * degree + 128] * scale).astype(BF)
    for m, ref, w in ((1, one_in, w4), (2, two_in, w5)):
        u = dot(ref[...], w[...])
        for degree in range(m, DEGREE + 1):
            scale = 1.0 / math.sqrt(2 * degree + 1)
            at = FIRST_KEPT[degree] + spread_of(degree)
            c = 128 * (degree - m)
            turned[at + m] = (u[:EDGES, c : c + 128] * scale).astype(BF)
            turned[at - m] = (u[EDGES:, c : c + 128] * scale).astype(BF)

    def turn_out(group, carry):
        at = pl.ds(pl.multiple_of(group * GROUP, GROUP), GROUP)
        for degree in range(DEGREE + 1):
            first, width, n = FIRST_KEPT[degree], 2 * degree + 1, kept(degree)
            result = dot(
                outof[degree * degree : degree * degree + width, at, :]
                .reshape(width * GROUP, 128)[:, : n * GROUP],
                turned[first : first + n, at, :].reshape(n * GROUP, 128),
            )
            edges[degree * degree : degree * degree + width, at, :] = result.astype(BF).reshape(
                width, GROUP, 128
            )
        return carry

    lax.fori_loop(0, GROUPS, turn_out, 0)
    lane = lax.broadcasted_iota(jnp.int32, (160, EDGES), 1)
    cells = cell_numbers((160, EDGES))
    scatter = jnp.where(
        (cells == target_ref[...]) & (lane < count_ref[0, 0]), 1.0, 0.0
    ).astype(BF)

    def deposit(step, carry):
        rows = jnp.concatenate([edges[step * 7 + n] for n in range(7)], 1)
        total = dot(scatter, rows)
        for n in range(7):
            comp = step * 7 + n
            part = total[:, 128 * n : 128 * n + 128]
            own_out[:, comp] = part[:64].reshape(4, 16, 128)
            slab_out[:, comp] = part[64:128].reshape(4, 16, 128)
            left_out[comp] = part[128:144].astype(BF)
            right_out[comp] = part[144:160].astype(BF)
        return carry

    lax.fori_loop(0, 7, deposit, 0)


def compute(own, slab, left, right, source, target, turn, count, table, weights):
    vmem = pl.BlockSpec(memory_space=pltpu.VMEM)
    smem = pl.BlockSpec(memory_space=pltpu.SMEM)
    anywhere = pl.BlockSpec(memory_space=pl.ANY)
    into = [
        pltpu.VMEM((kept(d), EDGES, 128 if d <= 3 else 256), BF) for d in range(DEGREE + 1)
    ]
    return pl.pallas_call(
        compute_kernel,
        out_shape=(
            jax.ShapeDtypeStruct((4, COMPS, 16, 128), F32),
            jax.ShapeDtypeStruct((4, COMPS, 16, 128), F32),
            jax.ShapeDtypeStruct((COMPS, 16, 128), BF),
            jax.ShapeDtypeStruct((COMPS, 16, 128), BF),
        ),
        in_specs=[vmem] * 7 + [smem, vmem] + [anywhere] * 6,
        out_specs=(vmem,) * 4,
        scratch_shapes=[pltpu.VMEM(w.shape, BF) for w in weights]
        + [pltpu.VMEM((EDGES, 1024), BF), pltpu.VMEM((128, 2048), BF)]
        + into
        + [
            pltpu.VMEM((COMPS, EDGES, 128), BF),
            pltpu.VMEM((EDGES, 160), BF),
            pltpu.VMEM((COMPS, EDGES, 128), BF),
            pltpu.VMEM((EDGES, 896), BF),
            pltpu.VMEM((2 * EDGES, 1536), BF),
            pltpu.VMEM((2 * EDGES, 1280), BF),
            pltpu.VMEM((FIRST_KEPT[-1], EDGES, 128), BF),
            pltpu.SemaphoreType.DMA((6,)),
        ],
        compiler_params=pltpu.CompilerParams(vmem_limit_bytes=60 * 1024 * 1024),
        cost_estimate=pl.CostEstimate(
            flops=12_000_000_000, bytes_accessed=20_000_000, transcendentals=40_000
        ),
        name="edge_messages",
    )(own, slab, left, right, source, target, turn, count, table, *weights)


def ring(axis, step):
    n = lax.axis_size(axis)
    return [(i, (i + step) % n) for i in range(n)]


def shift(x, axis, step):
    return lax.ppermute(x, axis, ring(axis, step))


def to_side(rows):
    return jnp.transpose(rows, (1, 0, 2, 3)).reshape(COMPS, 16, 128)


def from_side(side):
    return jnp.transpose(side.reshape(COMPS, 8, 2, 128), (1, 0, 2, 3))


def shards(features, source_cell, target_cell, rotation, edge_count, *weights):
    own = jnp.transpose(features, (0, 2, 1, 3))
    turn = jnp.transpose(rotation[0, 0], (2, 0, 1)).reshape(WIGNER, EDGES)
    weights = [w.reshape(-1, w.shape[-1]) for w in weights]
    low = shift(own[2:], "slab", 1)
    high = shift(own[:2], "slab", -1)
    tall = jnp.concatenate([low, own, high], 0)
    left = shift(to_side(tall[:, :, 14:]), "sub", 1)
    right = shift(to_side(tall[:, :, :2]), "sub", -1)
    slab = jnp.concatenate([low, high], 0)
    own_sum, slab_sum, left_sum, right_sum = compute(
        own,
        slab,
        left,
        right,
        source_cell.reshape(1, EDGES),
        target_cell.reshape(1, EDGES),
        turn,
        edge_count,
        jnp.asarray(entry_tables()),
        weights,
    )
    from_right = from_side(shift(left_sum, "sub", -1)).astype(F32)
    from_left = from_side(shift(right_sum, "sub", 1)).astype(F32)
    side = jnp.pad(from_right, ((0, 0), (0, 0), (14, 0), (0, 0))) + jnp.pad(
        from_left, ((0, 0), (0, 0), (0, 14), (0, 0))
    )
    slab_sum = (slab_sum + jnp.concatenate([side[:2], side[6:]], 0)).astype(BF)
    from_high = shift(slab_sum[:2], "slab", -1).astype(F32)
    from_low = shift(slab_sum[2:], "slab", 1).astype(F32)
    total = own_sum + side[2:6] + jnp.concatenate([from_low, from_high], 0)
    return jnp.transpose(total.astype(BF), (0, 2, 1, 3))


def solution(mesh):
    return jax.shard_map(
        shards,
        mesh=mesh,
        in_specs=(
            P("slab", "sub", None, None),
            P("slab", "sub", None, None),
            P("slab", "sub", None, None),
            P("slab", "sub", None, None, None),
            P("slab", "sub"),
            P(),
            P(),
            P(),
            P(),
            P(),
            P(),
        ),
        out_specs=P("slab", "sub", None, None),
        check_vma=False,
    )
```

time: 240 us -> 76.6 us (0.32)
  waiting for transfers between devices: 114 us -> 28.4 us
  local copies, waits for them, and re-layouts: 50.8 us -> 3.65 us
  matrix products: 23.5 us -> 0 us
  Pallas kernels: 0 us -> 22.9 us
  other arithmetic: 23.7 us -> 3.47 us
  starting transfers between devices: 24.8 us -> 17.3 us
    ppermute x8, waiting for transfers between devices: 114 us -> 28.4 us  [shift(): return lax.ppermute(x, axis, ring(axis, step))]
    dot_general x23 -> x0, matrix products: 23.5 us -> none  [the longest x4 6.32 us: convolve(): former = jnp.dot(pair_in, w_pair[0], preferred_element_type=jnp.float32)]
    pallas_call x0 -> x1, Pallas kernels: none -> 22.9 us  [compute(): pl.pallas_call(compute_kernel, out_shape=(jax.ShapeDtypeStruct((4, COMPS,...]
    while x69 -> x0, local copies, waits for them, and re-layouts: 8.9 us -> none
    reshape x13 -> x0, local copies, waits for them, and re-layouts: 7.87 us -> none  [the longest x1 4.98 us: fold_back(): collected.reshape(own_rows + 2 * REACH, own_cols + 2 * REACH, components...]
    ppermute x8, starting transfers between devices: 24.8 us -> 17.3 us  [shift(): return lax.ppermute(x, axis, ring(axis, step))]
    slice x16 -> x2, local copies, waits for them, and re-layouts: 8.65 us -> 1.47 us  [the longest x1 1.33 us: shards(): low = shift(own[2:], 'slab', 1)]
    scatter-add x4 -> x0, other arithmetic: 6.42 us -> none  [the longest x1 2.52 us: fold_rows(): folded = folded.at[own_rows:own_rows + REACH].add(arrived)]
  transfers between devices with their start and end apart: 8 -> 8, of which waited for: 6 -> 5; matrix products, arithmetic and copies ran while one was open for 6% -> 3% of each run, Pallas kernels for 0% -> 0%
where the time goes in v1:
time: 76.6 us; the launch traced here: 76.5 us
  waiting for transfers between devices  28.4 us (37%)
  Pallas kernels  22.9 us (30%)
  starting transfers between devices  17.3 us (23%)
  local copies, waits for them, and re-layouts  3.65 us (5%)
  other arithmetic  3.47 us (5%)
  between operations  0.81 us (1%)
    ppermute x8, waiting for transfers between devices, shift(): return lax.ppermute(x, axis, ring(axis, step))  28.4 us
    pallas_call x1, Pallas kernels, compute(): pl.pallas_call(compute_kernel, out_shape=(jax.ShapeDtypeStruct((4, COMPS,...  22.9 us
    ppermute x8, starting transfers between devices, shift(): return lax.ppermute(x, axis, ring(axis, step))  17.3 us
    unnamed x14, local copies, waits for them, and re-layouts  1.62 us
  transfers between devices with their start and end apart: 8, of which 5 were waited for; matrix products, arithmetic and copies ran while one was open for 3% of the time, Pallas kernels for 0%

profile of v1, /device:TPU:7, one launch (start us, length us, event | category | flops | bytes accessed | tf_op | source)
XLA Modules:
  0.0 76.5 jit_solution(308982482823492489)
XLA Ops:
  0.0 1.3 %fusion.6 = (bf16[2,49,16,128]{3,2,1,0:T(8,128)(2,1)S(1)}, bf16[2,49,16,128]{3,2,1,0:T(8,128)(2,1)S(1)}) fusion(bf16[4,49,16,128]{3,2,1,0:T(8,128)(2,1)} %bitcast.29), kind=kLoop, calls=%fused_computation.17 | loop fusion | bytes 1605632 | tf_op jit(solution)/shard_map/slice | solution.py:343
  1.4 1.7 %collective-permute-start = (bf16[2,49,16,128]{3,2,1,0:T(8,128)(2,1)S(1)}, bf16[2,49,16,128]{3,2,1,0:T(8,128)(2,1)S(1)}, u32[]{:S(2)}, u32[]{:S(2)}) collective-permute-start(bf16[2,49,16,128]{3,2,1,0:T(8,128)(2,1)S(1)} %get-tuple-element.17), channel_id=1, source_target_pairs={{0,16},{16,32},{32,48},{48,64},{64,80},{80,96},{96,112},{112,128},... | collective-permute-start | bytes 1204232 | tf_op jit(solution)/shard_map/ppermute | solution.py:328
  3.1 6.7 %collective-permute-start.1 = (bf16[2,49,16,128]{3,2,1,0:T(8,128)(2,1)S(1)}, bf16[2,49,16,128]{3,2,1,0:T(8,128)(2,1)S(1)}, u32[]{:S(2)}, u32[]{:S(2)}) collective-permute-start(bf16[2,49,16,128]{3,2,1,0:T(8,128)(2,1)S(1)} %get-tuple-element.18), channel_id=1, source_target_pairs={{0,240},{16,0},{32,16},{48,32},{64,48},{80,64},{96,80},{112,96},{1... | collective-permute-start | bytes 1204232 | tf_op jit(solution)/shard_map/ppermute | solution.py:328
  9.7 8.9 %collective-permute-done = bf16[2,49,16,128]{3,2,1,0:T(8,128)(2,1)S(1)} collective-permute-done((bf16[2,49,16,128]{3,2,1,0:T(8,128)(2,1)S(1)}, bf16[2,49,16,128]{3,2,1,0:T(8,128)(2,1)S(1)}, u32[]{:S(2)}, u32[]{:S(2)}) %collective-permute-start) | collective-permute-done | bytes 401440 | tf_op jit(solution)/shard_map/ppermute | solution.py:328
  18.6 0.3 fusion.4
  19.0 0.1 copy.14
  19.1 0.1 copy.13
  19.2 1.6 %collective-permute-start.2 = (bf16[49,16,128]{2,1,0:T(8,128)(2,1)S(1)}, bf16[49,16,128]{2,1,0:T(8,128)(2,1)S(1)}, u32[]{:S(2)}, u32[]{:S(2)}) collective-permute-start(bf16[49,16,128]{2,1,0:T(8,128)(2,1)S(1)} %bitcast.40), channel_id=1, source_target_pairs={{0,1},{1,2},{2,3},{3,4},{4,5},{5,6},{6,7},{7,8},{8,9},{9,10},{10,1... | collective-permute-start | bytes 602120 | tf_op jit(solution)/shard_map/ppermute | solution.py:328
  21.5 0.2 pad.41
  21.7 0.7 copy.17
  22.4 1.0 %pad_maximum_fusion.slab_ref = bf16[4,49,16,128]{3,2,1,0:T(8,128)(2,1)} fusion(bf16[2,49,16,128]{3,2,1,0:T(8,128)(2,1)S(1)} %collective-permute-done.1, bf16[2,49,16,128]{3,2,1,0:T(8,128)(2,1)S(1)} %collective-permute-done), kind=kLoop, calls=%fused_computation.9 | loop fusion | flops 401408 | bytes 1605632 | tf_op jit(solution)/shard_map/concatenate | solution.py:348
  23.5 4.6 %collective-permute-done.3.right_ref = bf16[49,16,128]{2,1,0:T(8,128)(2,1)S(1)} collective-permute-done((bf16[49,16,128]{2,1,0:T(8,128)(2,1)S(1)}, bf16[49,16,128]{2,1,0:T(8,128)(2,1)S(1)}, u32[]{:S(2)}, u32[]{:S(2)}) %collective-permute-start.3) | collective-permute-done | bytes 200736 | tf_op jit(solution)/shard_map/ppermute | solution.py:328
  28.1 0.7 copy-done.5
  28.8 22.9 %edge_messages.1 = (f32[4,49,16,128]{3,2,1,0:T(8,128)}, f32[4,49,16,128]{3,2,1,0:T(8,128)}, bf16[49,16,128]{2,1,0:T(8,128)(2,1)}, bf16[49,16,128]{2,1,0:T(8,128)(2,1)}) custom-call(bf16[4,49,16,128]{3,2,1,0:T(8,128)(2,1)} %bitcast.30, bf16[4,49,16,128]{3,2,1,0:T(8,128)(2,1)} %pad_maximum_fusion.slab_ref, bf16[49,16,128]{2,1,0:T(8,128)(2,1)} %copy-done.4, ...), custom_call_target="tpu_custom_call" | custom-call | flops 12000000000 | bytes 20000000 | tf_op jit(solution)/shard_map/edge_messages/pallas_call | solution.py:291
  51.7 0.3 collective-permute-start.4
  51.9 1.7 %collective-permute-start.5 = (bf16[49,16,128]{2,1,0:T(8,128)(2,1)}, bf16[49,16,128]{2,1,0:T(8,128)(2,1)S(1)}, u32[]{:S(2)}, u32[]{:S(2)}) collective-permute-start(bf16[49,16,128]{2,1,0:T(8,128)(2,1)} %get-tuple-element.11), channel_id=1, source_target_pairs={{0,1},{1,2},{2,3},{3,4},{4,5},{5,6},{6,7},{7,8},{8,9},{9,10},{10,1... | collective-permute-start | bytes 602120 | tf_op jit(solution)/shard_map/ppermute | solution.py:328
  53.7 5.8 %collective-permute-done.4 = bf16[49,16,128]{2,1,0:T(8,128)(2,1)S(1)} collective-permute-done((bf16[49,16,128]{2,1,0:T(8,128)(2,1)}, bf16[49,16,128]{2,1,0:T(8,128)(2,1)S(1)}, u32[]{:S(2)}, u32[]{:S(2)}) %collective-permute-start.4) | collective-permute-done | bytes 200736 | tf_op jit(solution)/shard_map/ppermute | solution.py:328
  59.6 0.1 copy.20
  59.7 0.2 convert_add_fusion.2
  60.0 0.2 fusion.2
  60.4 5.2 %collective-permute-start.7 = (bf16[2,49,16,128]{3,2,1,0:T(8,128)(2,1)S(1)}, bf16[2,49,16,128]{3,2,1,0:T(8,128)(2,1)S(1)}, u32[]{:S(2)}, u32[]{:S(2)}) collective-permute-start(bf16[2,49,16,128]{3,2,1,0:T(8,128)(2,1)S(1)} %get-tuple-element.16), channel_id=1, source_target_pairs={{0,240},{16,0},{32,16},{48,32},{64,48},{80,64},{96,80},{112,96},{1... | collective-permute-start | bytes 1204232 | tf_op jit(solution)/shard_map/ppermute | solution.py:328
  65.7 0.5 convert_add_fusion
  66.1 9.0 %collective-permute-done.6 = bf16[2,49,16,128]{3,2,1,0:T(8,128)(2,1)S(1)} collective-permute-done((bf16[2,49,16,128]{3,2,1,0:T(8,128)(2,1)S(1)}, bf16[2,49,16,128]{3,2,1,0:T(8,128)(2,1)S(1)}, u32[]{:S(2)}, u32[]{:S(2)}) %collective-permute-start.6) | collective-permute-done | bytes 401440 | tf_op jit(solution)/shard_map/ppermute | solution.py:328
  75.2 1.3 %fusion.3 = bf16[4,16,49,128]{3,1,2,0:T(8,128)(2,1)} fusion(f32[4,49,16,128]{3,2,1,0:T(8,128)S(1)} %copy-done.1, f32[8,49,16,128]{3,2,1,0:T(8,128)S(1)} %convert_add_fusion, bf16[2,49,16,128]{3,2,1,0:T(8,128)(2,1)S(1)} %collective-permute-done.7, bf16[2,49,16,128]{3,2,1,0:T(8,128)(2,1)S(1)} %collective-permute-done.6), kind=kLoop, calls=%fused_computation.6 | loop fusion | flops 2007040 | bytes 4816896 | tf_op jit(solution)/shard_map/transpose | solution.py:370
  (19 shorter events, 0.5 us)
Async XLA Ops:
  0.0 18.6 %copy-start = (bf16[4,16,49,128]{3,1,2,0:T(8,128)(2,1)S(1)}, bf16[4,16,49,128]{3,1,2,0:T(8,128)(2,1)}, u32[]{:S(2)}) copy-start(bf16[4,16,49,128]{3,1,2,0:T(8,128)(2,1)} %param.12) | copy-start | bytes 2408452
  1.3 20.2 %copy-start.3 = (bf16[1,1,2,128,455]{3,2,4,1,0:T(2,128)(2,1)S(1)}, bf16[1,1,2,128,455]{3,2,4,1,0:T(2,128)(2,1)}, u32[]{:S(2)}) copy-start(bf16[1,1,2,128,455]{3,2,4,1,0:T(2,128)(2,1)} %param.15) | copy-start | bytes 698884
  1.4 17.3 %collective-permute-start = (bf16[2,49,16,128]{3,2,1,0:T(8,128)(2,1)S(1)}, bf16[2,49,16,128]{3,2,1,0:T(8,128)(2,1)S(1)}, u32[]{:S(2)}, u32[]{:S(2)}) collective-permute-start(bf16[2,49,16,128]{3,2,1,0:T(8,128)(2,1)S(1)} %get-tuple-element.17), channel_id=1, source_target_pairs={{0,16},{16,32},{32,48},{48,64},{64,80},{80,96},{96,112},{112,128},... | collective-permute-start | bytes 1204232 | tf_op jit(solution)/shard_map/ppermute | solution.py:328
  3.1 15.6 %collective-permute-start.1 = (bf16[2,49,16,128]{3,2,1,0:T(8,128)(2,1)S(1)}, bf16[2,49,16,128]{3,2,1,0:T(8,128)(2,1)S(1)}, u32[]{:S(2)}, u32[]{:S(2)}) collective-permute-start(bf16[2,49,16,128]{3,2,1,0:T(8,128)(2,1)S(1)} %get-tuple-element.18), channel_id=1, source_target_pairs={{0,240},{16,0},{32,16},{48,32},{64,48},{80,64},{96,80},{112,96},{1... | collective-permute-start | bytes 1204232 | tf_op jit(solution)/shard_map/ppermute | solution.py:328
  19.2 4.3 %collective-permute-start.2 = (bf16[49,16,128]{2,1,0:T(8,128)(2,1)S(1)}, bf16[49,16,128]{2,1,0:T(8,128)(2,1)S(1)}, u32[]{:S(2)}, u32[]{:S(2)}) collective-permute-start(bf16[49,16,128]{2,1,0:T(8,128)(2,1)S(1)} %bitcast.40), channel_id=1, source_target_pairs={{0,1},{1,2},{2,3},{3,4},{4,5},{5,6},{6,7},{7,8},{8,9},{9,10},{10,1... | collective-permute-start | bytes 602120 | tf_op jit(solution)/shard_map/ppermute | solution.py:328
  20.9 7.2 %collective-permute-start.3 = (bf16[49,16,128]{2,1,0:T(8,128)(2,1)S(1)}, bf16[49,16,128]{2,1,0:T(8,128)(2,1)S(1)}, u32[]{:S(2)}, u32[]{:S(2)}) collective-permute-start(bf16[49,16,128]{2,1,0:T(8,128)(2,1)S(1)} %bitcast.39), channel_id=1, source_target_pairs={{0,15},{1,0},{2,1},{3,2},{4,3},{5,4},{6,5},{7,6},{8,7},{9,8},{10,9... | collective-permute-start | bytes 602120 | tf_op jit(solution)/shard_map/ppermute | solution.py:328
  23.5 4.6 %copy-start.4 = (bf16[49,16,128]{2,1,0:T(8,128)(2,1)}, bf16[49,16,128]{2,1,0:T(8,128)(2,1)S(1)}, u32[]{:S(2)}) copy-start(bf16[49,16,128]{2,1,0:T(8,128)(2,1)S(1)} %collective-permute-done.2.left_ref) | copy-start | bytes 602116
  28.1 0.7 copy-start.5
  51.7 8.3 %copy-start.2 = (f32[4,49,16,128]{3,2,1,0:T(8,128)S(1)}, f32[4,49,16,128]{3,2,1,0:T(8,128)}, u32[]{:S(2)}) copy-start(f32[4,49,16,128]{3,2,1,0:T(8,128)} %get-tuple-element.12) | copy-start | bytes 4816900
  51.7 7.8 %collective-permute-start.4 = (bf16[49,16,128]{2,1,0:T(8,128)(2,1)}, bf16[49,16,128]{2,1,0:T(8,128)(2,1)S(1)}, u32[]{:S(2)}, u32[]{:S(2)}) collective-permute-start(bf16[49,16,128]{2,1,0:T(8,128)(2,1)} %get-tuple-element.10), channel_id=1, source_target_pairs={{0,15},{1,0},{2,1},{3,2},{4,3},{5,4},{6,5},{7,6},{8,7},{9,8},{10,9... | collective-permute-start | bytes 602120 | tf_op jit(solution)/shard_map/ppermute | solution.py:328
  51.9 7.6 %collective-permute-start.5 = (bf16[49,16,128]{2,1,0:T(8,128)(2,1)}, bf16[49,16,128]{2,1,0:T(8,128)(2,1)S(1)}, u32[]{:S(2)}, u32[]{:S(2)}) collective-permute-start(bf16[49,16,128]{2,1,0:T(8,128)(2,1)} %get-tuple-element.11), channel_id=1, source_target_pairs={{0,1},{1,2},{2,3},{3,4},{4,5},{5,6},{6,7},{7,8},{8,9},{9,10},{10,1... | collective-permute-start | bytes 602120 | tf_op jit(solution)/shard_map/ppermute | solution.py:328
  60.3 14.8 %collective-permute-start.6 = (bf16[2,49,16,128]{3,2,1,0:T(8,128)(2,1)S(1)}, bf16[2,49,16,128]{3,2,1,0:T(8,128)(2,1)S(1)}, u32[]{:S(2)}, u32[]{:S(2)}) collective-permute-start(bf16[2,49,16,128]{3,2,1,0:T(8,128)(2,1)S(1)} %get-tuple-element.15), channel_id=1, source_target_pairs={{0,16},{16,32},{32,48},{48,64},{64,80},{80,96},{96,112},{112,128},... | collective-permute-start | bytes 1204232 | tf_op jit(solution)/shard_map/ppermute | solution.py:328
  60.4 14.8 %copy-start.1 = (f32[4,49,16,128]{3,2,1,0:T(8,128)S(1)}, f32[4,49,16,128]{3,2,1,0:T(8,128)}, u32[]{:S(2)}) copy-start(f32[4,49,16,128]{3,2,1,0:T(8,128)} %get-tuple-element.9) | copy-start | bytes 4816900
  60.4 14.7 %collective-permute-start.7 = (bf16[2,49,16,128]{3,2,1,0:T(8,128)(2,1)S(1)}, bf16[2,49,16,128]{3,2,1,0:T(8,128)(2,1)S(1)}, u32[]{:S(2)}, u32[]{:S(2)}) collective-permute-start(bf16[2,49,16,128]{3,2,1,0:T(8,128)(2,1)S(1)} %get-tuple-element.16), channel_id=1, source_target_pairs={{0,240},{16,0},{32,16},{48,32},{64,48},{80,64},{96,80},{112,96},{1... | collective-permute-start | bytes 1204232 | tf_op jit(solution)/shard_map/ppermute | solution.py:328

commit v2 on v1

v2 whole, which is shorter than its diff:
```python
import math

import jax
import jax.numpy as jnp
import numpy as np
from jax import lax
from jax.experimental import pallas as pl
from jax.experimental.pallas import tpu as pltpu
from jax.sharding import PartitionSpec as P

DEGREE = 6
REACH = 2
COMPS = 49
WIGNER = 455
EDGES = 256
GROUP = 16
GROUPS = EDGES // GROUP
BF = jnp.bfloat16
F32 = jnp.float32


def spread_of(degree):
    return min(degree, 2)


def kept(degree):
    return 2 * spread_of(degree) + 1


FIRST_KEPT = [sum(kept(k) for k in range(d)) for d in range(DEGREE + 2)]
OFFSETS = [sum((2 * k + 1) ** 2 for k in range(d)) for d in range(DEGREE + 1)]


def entry_tables():
    inward = np.full((512,), -1, np.int32)
    outward = np.full((512,), -1, np.int32)
    row = 0
    for degree in range(DEGREE + 1):
        width = 2 * degree + 1
        spread = spread_of(degree)
        for slot, i in enumerate(range(degree - spread, degree + spread + 1)):
            for j in range(width):
                entry = OFFSETS[degree] + i * width + j
                inward[16 * row + j] = entry
                outward[8 * (degree * degree + j) + slot] = entry
            row += 1
    return np.concatenate([inward, outward])[None, :]


def transposed_dot(a, b):
    return lax.dot_general(a, b, (((0,), (0,)), ((), ())), preferred_element_type=F32)


def dot(a, b):
    return jnp.dot(a, b, preferred_element_type=F32)


def expand_rotations(table_ref, turn_ref, padded, grid_map, into, outof):
    wanted = table_ref[...]
    rows = lax.broadcasted_iota(jnp.int32, (WIGNER, 1024), 0)
    pick = jnp.where(rows == wanted, 1.0, 0.0).astype(BF)
    padded[...] = transposed_dot(turn_ref[...], pick).astype(BF)
    k = lax.broadcasted_iota(jnp.int32, (128, 2048), 0)
    col = lax.broadcasted_iota(jnp.int32, (128, 2048), 1)
    grid_map[...] = jnp.where(k == (col >> 4), 1.0, 0.0).astype(BF)
    edge = lax.broadcasted_iota(jnp.int32, (EDGES, 256), 0)
    lane = lax.broadcasted_iota(jnp.int32, (EDGES, 256), 1)
    own = (edge & 15) == (lane & 15)
    for degree in range(DEGREE + 1):
        lanes = 128 if degree <= 3 else 256
        for slot in range(kept(degree)):
            row = FIRST_KEPT[degree] + slot
            block = dot(
                padded[:, 128 * (row // 8) : 128 * (row // 8) + 128],
                grid_map[:, 256 * (row % 8) : 256 * (row % 8) + lanes],
            )
            into[degree][slot] = jnp.where(own[:, :lanes], block, 0.0).astype(BF)
    for pair in range((COMPS + 1) // 2):
        chunk, place = pair // 8, pair % 8
        block = dot(
            padded[:, 512 + 128 * chunk : 640 + 128 * chunk],
            grid_map[:, 256 * place : 256 * place + 256],
        )
        block = jnp.where(own, block, 0.0).astype(BF)
        outof[2 * pair] = block[:, :128]
        if 2 * pair + 1 < COMPS:
            outof[2 * pair + 1] = block[:, 128:]


def cell_numbers(shape, dim):
    k = lax.broadcasted_iota(jnp.int32, shape, dim)
    own = ((k >> 4) + 2) * 20 + (k & 15) + 2
    r = (k - 64) >> 4
    slab = (jnp.where(r < 2, r, r + 4)) * 20 + (k & 15) + 2
    s = (k - 128) & 15
    side = (s >> 1) * 20 + (s & 1) + jnp.where(k >= 144, 18, 0)
    return jnp.where(k < 64, own, jnp.where(k < 128, slab, side))


def rim_map(shape, cell_dim):
    cells = cell_numbers(shape, cell_dim)
    s = lax.broadcasted_iota(jnp.int32, shape, 1 - cell_dim)
    wanted = ((s & 15) >> 1) * 20 + (s & 1) + jnp.where(s < 16, 16, 2)
    return jnp.where(cells == wanted, 1.0, 0.0).astype(BF)


MESH = pl.DeviceIdType.MESH
IN_CHUNKS = ((6, 6), (0, 3), (5, 5), (4, 4))
OUT_CHUNKS = ((6, 6), (4, 5), (0, 3))
STEP = 4


def comps_of(chunk):
    return chunk[0] ** 2, (chunk[1] + 1) ** 2


def steps_of(chunk):
    lo, hi = comps_of(chunk)
    return [range(c, min(c + STEP, hi)) for c in range(lo, hi, STEP)]


def fused_kernel(
    own_hbm,
    source_ref,
    target_ref,
    turn_ref,
    count_ref,
    table_ref,
    w0_hbm,
    w1_hbm,
    w2_hbm,
    w3_hbm,
    w4_hbm,
    w5_hbm,
    out,
    own,
    slab,
    side,
    rim,
    w0,
    w1,
    w2,
    w3,
    w4,
    w5,
    padded,
    grid_map,
    i0,
    i1,
    i2,
    i3,
    i4,
    i5,
    i6,
    outof,
    gather_map,
    edges,
    zero_in,
    one_in,
    two_in,
    turned,
    summed,
    side_out,
    side_back,
    slab_out,
    slab_back,
    sem,
    in_sem,
    out_sem,
):
    into = (i0, i1, i2, i3, i4, i5, i6)
    load_own = pltpu.make_async_copy(own_hbm, own, sem.at[6])
    load_own.start()
    weights = [
        pltpu.make_async_copy(src, dst, sem.at[n])
        for n, (src, dst) in enumerate(
            ((w0_hbm, w0), (w1_hbm, w1), (w2_hbm, w2), (w3_hbm, w3), (w4_hbm, w4), (w5_hbm, w5))
        )
    ]
    a, b = lax.axis_index("slab"), lax.axis_index("sub")
    rows, cols = lax.axis_size("slab"), lax.axis_size("sub")
    up, down = (lax.rem(a + 1, rows), b), (lax.rem(a + rows - 1, rows), b)
    right, left = (a, lax.rem(b + 1, cols)), (a, lax.rem(b + cols - 1, cols))
    barrier = pltpu.get_barrier_semaphore()
    for there in (up, down, right, left):
        pl.semaphore_signal(barrier, inc=1, device_id=there, device_id_type=MESH)
    pl.semaphore_wait(barrier, 4)
    load_own.wait()

    sent = []

    def send(source, target, sems, kind, n, there):
        copy = pltpu.make_async_remote_copy(
            src_ref=source,
            dst_ref=target,
            send_sem=sems.at[0, kind, n],
            recv_sem=sems.at[1, kind, n],
            device_id=there,
            device_id_type=MESH,
        )
        copy.start()
        sent.append(copy)
        return copy

    slab_in = []
    for n, chunk in enumerate(IN_CHUNKS):
        lo, hi = comps_of(chunk)
        slab_in.append(
            (
                send(own.at[2:4, lo:hi], slab.at[0:2, lo:hi], in_sem, 0, n, up),
                send(own.at[0:2, lo:hi], slab.at[2:4, lo:hi], in_sem, 1, n, down),
            )
        )
    for copy in weights:
        copy.start()
    expand_rotations(table_ref, turn_ref, padded, grid_map, into, outof)
    cells = cell_numbers((160, EDGES), 0)
    to_target = jnp.where(cells == target_ref[...], 1.0, 0.0)
    both = to_target + jnp.where(cells == source_ref[...], 1.0, 0.0)
    gather_map[...] = both.T.astype(BF)

    def send_rim(n):
        for copy in slab_in[n]:
            copy.wait_recv()
        take = rim_map((32, 128), 1)
        for step in steps_of(IN_CHUNKS[n]):
            tall = [
                jnp.concatenate([own[:, c].reshape(64, 128), slab[:, c].reshape(64, 128)], 0)
                for c in step
            ]
            got = dot(take, jnp.concatenate(tall, 1)).astype(BF)
            for k, c in enumerate(step):
                rim[0, c] = got[:16, 128 * k : 128 * k + 128]
                rim[1, c] = got[16:, 128 * k : 128 * k + 128]
        lo, hi = comps_of(IN_CHUNKS[n])
        return (
            send(rim.at[0, lo:hi], side.at[0, lo:hi], in_sem, 2, n, right),
            send(rim.at[1, lo:hi], side.at[1, lo:hi], in_sem, 3, n, left),
        )

    def gather(chunk):
        for step in steps_of(chunk):
            pieces = [
                jnp.concatenate(
                    [
                        own[:, c].reshape(64, 128),
                        slab[:, c].reshape(64, 128),
                        side[0, c],
                        side[1, c],
                    ],
                    0,
                )
                for c in step
            ]
            total = dot(gather_map[...], jnp.concatenate(pieces, 1)).astype(BF)
            for k, c in enumerate(step):
                edges[c] = total[:, 128 * k : 128 * k + 128]

    def turn_in(chunk):
        def group_pair(pair, carry):
            for group in (2 * pair, 2 * pair + 1):
                at = pl.ds(pl.multiple_of(group * GROUP, GROUP), GROUP)
                low = pl.ds(pl.multiple_of(EDGES + group * GROUP, GROUP), GROUP)
                for degree in range(chunk[0], chunk[1] + 1):
                    width = 2 * degree + 1
                    n = kept(degree)
                    values = edges[degree * degree : degree * degree + width, at, :]
                    result = dot(
                        into[degree][:, at, :].reshape(n * GROUP, -1)[:, : width * GROUP],
                        values.reshape(width * GROUP, 128),
                    )
                    result = result * (1.0 / math.sqrt(width))
                    piece = [result[GROUP * k : GROUP * k + GROUP] for k in range(n)]
                    mid = n // 2
                    zero_in[at, 128 * degree : 128 * degree + 128] = piece[mid].astype(BF)
                    for m, ref, half in ((1, one_in, 768), (2, two_in, 640)):
                        if degree < m:
                            continue
                        c = 128 * (degree - m)
                        plus, minus = piece[mid + m].astype(BF), piece[mid - m]
                        ref[at, c : c + 128] = plus
                        ref[at, half + c : half + c + 128] = (-minus).astype(BF)
                        ref[low, c : c + 128] = minus.astype(BF)
                        ref[low, half + c : half + c + 128] = plus
            return carry

        lax.fori_loop(0, GROUPS // 2, group_pair, 0)

    side_in = [send_rim(0)]
    for n, chunk in enumerate(IN_CHUNKS):
        if n + 1 < len(IN_CHUNKS):
            side_in.append(send_rim(n + 1))
        for copy in side_in[n]:
            copy.wait_recv()
        gather(chunk)
        turn_in(chunk)

    for copy in weights[:3]:
        copy.wait()
    y0 = dot(zero_in[...], w0[...])
    scalar = y0[:, :128]
    gate = jax.nn.sigmoid(scalar)
    y1 = dot(one_in[...], w1[...])
    zero_in[:, :128] = (scalar * gate).astype(BF)
    for degree in range(1, DEGREE + 1):
        c = 128 * degree
        zero_in[:, c : c + 128] = (y0[:, c : c + 128] * gate).astype(BF)
    y2 = dot(two_in[...], w2[...])
    for y, ref, half in ((y1, one_in, 768), (y2, two_in, 640)):
        for c in range(0, half, 128):
            plus = y[:EDGES, c : c + 128] * gate
            minus = y[EDGES:, c : c + 128] * gate
            ref[:EDGES, c : c + 128] = plus.astype(BF)
            ref[:EDGES, half + c : half + c + 128] = (-minus).astype(BF)
            ref[EDGES:, c : c + 128] = minus.astype(BF)
            ref[EDGES:, half + c : half + c + 128] = plus.astype(BF)
    for copy in weights[3:]:
        copy.wait()

    def second(chunk):
        for m, ref, w in ((0, zero_in, w3), (1, one_in, w4), (2, two_in, w5)):
            first = max(chunk[0], m)
            u = dot(ref[...], w[:, 128 * (first - m) : 128 * (chunk[1] + 1 - m)])
            for degree in range(first, chunk[1] + 1):
                scale = 1.0 / math.sqrt(2 * degree + 1)
                at = FIRST_KEPT[degree] + spread_of(degree)
                c = 128 * (degree - first)
                turned[at + m] = (u[:EDGES, c : c + 128] * scale).astype(BF)
                if m:
                    turned[at - m] = (u[EDGES:, c : c + 128] * scale).astype(BF)

    def turn_out(chunk):
        def group_pair(pair, carry):
            for group in (2 * pair, 2 * pair + 1):
                at = pl.ds(pl.multiple_of(group * GROUP, GROUP), GROUP)
                for degree in range(chunk[0], chunk[1] + 1):
                    first, width, n = FIRST_KEPT[degree], 2 * degree + 1, kept(degree)
                    result = dot(
                        outof[degree * degree : degree * degree + width, at, :]
                        .reshape(width * GROUP, 128)[:, : n * GROUP],
                        turned[first : first + n, at, :].reshape(n * GROUP, 128),
                    )
                    edges[degree * degree : degree * degree + width, at, :] = result.astype(
                        BF
                    ).reshape(width, GROUP, 128)
            return carry

        lax.fori_loop(0, GROUPS // 2, group_pair, 0)

    lane = lax.broadcasted_iota(jnp.int32, (160, EDGES), 1)
    cells = cell_numbers((160, EDGES), 0)
    scatter = jnp.where(
        (cells == target_ref[...]) & (lane < count_ref[0, 0]), 1.0, 0.0
    ).astype(BF)

    def deposit(n):
        for step in steps_of(OUT_CHUNKS[n]):
            total = dot(scatter, jnp.concatenate([edges[c] for c in step], 1))
            for k, c in enumerate(step):
                part = total[:, 128 * k : 128 * k + 128]
                summed[c] = part[:128]
                side_out[0, c] = part[128:144].astype(BF)
                side_out[1, c] = part[144:160].astype(BF)
        lo, hi = comps_of(OUT_CHUNKS[n])
        return (
            send(side_out.at[0, lo:hi], side_back.at[0, lo:hi], out_sem, 0, n, left),
            send(side_out.at[1, lo:hi], side_back.at[1, lo:hi], out_sem, 1, n, right),
        )

    def add_side(n):
        for copy in side_ret[n]:
            copy.wait_recv()
        spread = rim_map((128, 32), 0)
        for step in steps_of(OUT_CHUNKS[n]):
            got = jnp.concatenate(
                [jnp.concatenate([side_back[0, c], side_back[1, c]], 0) for c in step], 1
            )
            extra = dot(spread, got)
            for k, c in enumerate(step):
                total = summed[c] + extra[:, 128 * k : 128 * k + 128]
                summed[c, :64] = total[:64]
                slab_out[:, c] = total[64:].astype(BF).reshape(4, 16, 128)
        lo, hi = comps_of(OUT_CHUNKS[n])
        return (
            send(slab_out.at[0:2, lo:hi], slab_back.at[2:4, lo:hi], out_sem, 2, n, down),
            send(slab_out.at[2:4, lo:hi], slab_back.at[0:2, lo:hi], out_sem, 3, n, up),
        )

    side_ret, slab_ret = [], []
    for n, chunk in enumerate(OUT_CHUNKS):
        second(chunk)
        turn_out(chunk)
        side_ret.append(deposit(n))
        if n:
            slab_ret.append(add_side(n - 1))
    slab_ret.append(add_side(len(OUT_CHUNKS) - 1))
    for n, chunk in enumerate(OUT_CHUNKS):
        for copy in slab_ret[n]:
            copy.wait_recv()
        for c in range(*comps_of(chunk)):
            total = summed[c, :64] + slab_back[:, c].reshape(64, 128).astype(F32)
            out[:, c] = total.astype(BF).reshape(4, 16, 128)
    for copy in sent:
        copy.wait_send()


def fused(own, source, target, turn, count, table, weights):
    vmem = pl.BlockSpec(memory_space=pltpu.VMEM)
    smem = pl.BlockSpec(memory_space=pltpu.SMEM)
    anywhere = pl.BlockSpec(memory_space=pl.ANY)
    into = [
        pltpu.VMEM((kept(d), EDGES, 128 if d <= 3 else 256), BF) for d in range(DEGREE + 1)
    ]
    return pl.pallas_call(
        fused_kernel,
        out_shape=jax.ShapeDtypeStruct((4, COMPS, 16, 128), BF),
        in_specs=[anywhere] + [vmem] * 3 + [smem, vmem] + [anywhere] * 6,
        out_specs=vmem,
        scratch_shapes=[
            pltpu.VMEM((4, COMPS, 16, 128), BF),
            pltpu.VMEM((4, COMPS, 16, 128), BF),
            pltpu.VMEM((2, COMPS, 16, 128), BF),
            pltpu.VMEM((2, COMPS, 16, 128), BF),
        ]
        + [pltpu.VMEM(w.shape, BF) for w in weights]
        + [pltpu.VMEM((EDGES, 1024), BF), pltpu.VMEM((128, 2048), BF)]
        + into
        + [
            pltpu.VMEM((COMPS, EDGES, 128), BF),
            pltpu.VMEM((EDGES, 160), BF),
            pltpu.VMEM((COMPS, EDGES, 128), BF),
            pltpu.VMEM((EDGES, 896), BF),
            pltpu.VMEM((2 * EDGES, 1536), BF),
            pltpu.VMEM((2 * EDGES, 1280), BF),
            pltpu.VMEM((FIRST_KEPT[-1], EDGES, 128), BF),
            pltpu.VMEM((COMPS, 128, 128), F32),
            pltpu.VMEM((2, COMPS, 16, 128), BF),
            pltpu.VMEM((2, COMPS, 16, 128), BF),
            pltpu.VMEM((4, COMPS, 16, 128), BF),
            pltpu.VMEM((4, COMPS, 16, 128), BF),
            pltpu.SemaphoreType.DMA((7,)),
            pltpu.SemaphoreType.DMA((2, 4, len(IN_CHUNKS))),
            pltpu.SemaphoreType.DMA((2, 4, len(OUT_CHUNKS))),
        ],
        compiler_params=pltpu.CompilerParams(
            vmem_limit_bytes=52 * 1024 * 1024, collective_id=0, has_side_effects=True
        ),
        cost_estimate=pl.CostEstimate(
            flops=12_000_000_000, bytes_accessed=20_000_000, transcendentals=40_000
        ),
        name="edge_messages",
    )(own, source, target, turn, count, table, *weights)


def shards(features, source_cell, target_cell, rotation, edge_count, *weights):
    own = jnp.transpose(features, (0, 2, 1, 3))
    turn = jnp.transpose(rotation[0, 0], (2, 0, 1)).reshape(WIGNER, EDGES)
    weights = [w.reshape(-1, w.shape[-1]) for w in weights]
    result = fused(
        own,
        source_cell.reshape(1, EDGES),
        target_cell.reshape(1, EDGES),
        turn,
        edge_count,
        jnp.asarray(entry_tables()),
        weights,
    )
    return jnp.transpose(result, (0, 2, 1, 3))


def solution(mesh):
    return jax.shard_map(
        shards,
        mesh=mesh,
        in_specs=(
            P("slab", "sub", None, None),
            P("slab", "sub", None, None),
            P("slab", "sub", None, None),
            P("slab", "sub", None, None, None),
            P("slab", "sub"),
            P(),
            P(),
            P(),
            P(),
            P(),
            P(),
        ),
        out_specs=P("slab", "sub", None, None),
        check_vma=False,
    )
```

time: 76.6 us -> 64 us (0.84)
  the two profiles are of different devices: /device:TPU:7 before, /device:TPU:5 now
where the time goes in v2:
time: 64 us; the launch traced here: 63.8 us
  Pallas kernels  57.9 us (90%)
  local copies, waits for them, and re-layouts  5.22 us (8%)
  between operations  0.68 us (1%)
    pallas_call x1, Pallas kernels, fused(): pl.pallas_call(fused_kernel, out_shape=jax.ShapeDtypeStruct((4, COMPS, 16...  57.9 us
    unnamed x11, local copies, waits for them, and re-layouts  5.22 us

profile of v2, /device:TPU:5, one launch (start us, length us, event | category | flops | bytes accessed | tf_op | source)
XLA Modules:
  0.0 63.8 jit_solution(277148780960945323)
XLA Ops:
  0.7 1.1 %pad = bf16[456,2,128]{2,1,0:T(2,128)(2,1)S(1)} pad(bf16[455,2,128]{2,1,0:T(2,128)(2,1)} %bitcast.20, bf16[]{:T(256)} %constant.8), padding=0_1x0_0x0_0 | pad | bytes 466434
  1.8 0.0 copy-start
  1.8 1.1 %copy-done = bf16[4,16,49,128]{3,1,2,0:T(8,128)(2,1)S(1)} copy-done((bf16[4,16,49,128]{3,1,2,0:T(8,128)(2,1)S(1)}, bf16[4,16,49,128]{3,1,2,0:T(8,128)(2,1)}, u32[]{:S(2)}) %copy-start) | copy-done | bytes 802840
  3.0 0.0 copy-start.1
  3.0 0.7 %copy-done.1 = s32[1,1,2,128]{3,2,1,0:T(2,128)S(1)} copy-done((s32[1,1,2,128]{3,2,1,0:T(2,128)S(1)}, s32[1,1,2,128]{3,2,1,0:T(2,128)}, u32[]{:S(2)}) %copy-start.1) | copy-done | bytes 1048
  3.6 0.0 copy-start.2
  3.6 0.7 %copy-done.2 = s32[1,1,2,128]{3,2,1,0:T(2,128)S(1)} copy-done((s32[1,1,2,128]{3,2,1,0:T(2,128)S(1)}, s32[1,1,2,128]{3,2,1,0:T(2,128)}, u32[]{:S(2)}) %copy-start.2) | copy-done | bytes 1048
  4.3 0.0 copy-start.3
  4.3 0.7 %copy-done.3 = s32[1,1024]{1,0:T(1,128)S(1)} copy-done((s32[1,1024]{1,0:T(1,128)S(1)}, s32[1,1024]{1,0:T(1,128)}, u32[]{:S(2)}) %copy-start.3) | copy-done | bytes 4120
  5.0 57.9 %edge_messages.1 = bf16[4,49,16,128]{3,2,1,0:T(8,128)(2,1)S(1)} custom-call(bf16[4,49,16,128]{3,2,1,0:T(8,128)(2,1)S(1)} %bitcast.16, s32[1,256]{1,0:T(1,128)S(1)} %bitcast.17, s32[1,256]{1,0:T(1,128)S(1)} %bitcast.18, bf16[455,256]{1,0:T(8,128)(2,1)S(1)} %bitcast.15, s32[1,1]{1,0:T(1,128)S(6)} %copy.15.count_ref, s32[1,1024]{1,0:T(1,128)S(1)} %copy-done.3, ...), custom_call_target="tpu_custom_call" | custom-call | flops 12000000000 | bytes 20000000 | tf_op jit(solution)/shard_map/edge_messages/pallas_call | solution.py:414
  62.9 0.9 %copy.16 = bf16[4,16,49,128]{3,1,2,0:T(8,128)(2,1)} copy(bf16[4,16,49,128]{3,1,2,0:T(8,128)(2,1)S(1)} %bitcast.14) | data formatting | bytes 1605632
  (1 shorter events, 0.0 us)
Async XLA Ops:
  1.8 1.1 %copy-start = (bf16[4,16,49,128]{3,1,2,0:T(8,128)(2,1)S(1)}, bf16[4,16,49,128]{3,1,2,0:T(8,128)(2,1)}, u32[]{:S(2)}) copy-start(bf16[4,16,49,128]{3,1,2,0:T(8,128)(2,1)} %param.12) | copy-start | bytes 2408452
  3.0 0.7 %copy-start.1 = (s32[1,1,2,128]{3,2,1,0:T(2,128)S(1)}, s32[1,1,2,128]{3,2,1,0:T(2,128)}, u32[]{:S(2)}) copy-start(s32[1,1,2,128]{3,2,1,0:T(2,128)} %param.13) | copy-start | bytes 3076
  3.6 0.7 %copy-start.2 = (s32[1,1,2,128]{3,2,1,0:T(2,128)S(1)}, s32[1,1,2,128]{3,2,1,0:T(2,128)}, u32[]{:S(2)}) copy-start(s32[1,1,2,128]{3,2,1,0:T(2,128)} %param.14) | copy-start | bytes 3076
  4.3 0.7 %copy-start.3 = (s32[1,1024]{1,0:T(1,128)S(1)}, s32[1,1024]{1,0:T(1,128)}, u32[]{:S(2)}) copy-start(s32[1,1024]{1,0:T(1,128)} %constant.2.clone.table_ref) | copy-start | bytes 12292
